TPU v7x, 32 devices: a whole 2x2x4 slice. The times are simulated.
32 devices in a mesh: slab: 8 (over y, x, core), col: 4 (over z).
Axes of the slice: x: 2, y: 2, z: 4, core: 2. Of those that a mesh axis runs over, the one named last changes fastest.
Arguments:
- hamiltonian_blocks: bfloat16 [128, 9, 128, 128], P('slab'), may hold values from -0.0625 to 0.0625
- block_columns: int32 [128, 9], P('slab'), may hold values from 0 to 127, as said below
- probe: bfloat16 [16384, 2048], P('slab', 'col'), may hold values from -6 to 6
- previous: float32 [16384, 2048], P('slab', 'col'), may hold values from -6 to 6
- current: float32 [16384, 2048], P('slab', 'col'), may hold values from -6 to 6
- orbital_weight: float32 [16384], P('slab'), may hold values from 0.1 to 10
Outputs:
- last_previous: float32 [16384, 2048], P('slab', 'col')
- last_current: float32 [16384, 2048], P('slab', 'col')
- moments: float32 [3, 2048], P(None, 'col')
Inputs may be any that keep to these rules, and one draw needn't show every extreme that they name: `block_columns`: the 9 entries of a row are distinct block columns within 5 of the row's own block row, counted cyclically modulo 128; they include the row itself and the block rows 5 before and 5 after it.
All inputs are finite; a program needn't handle non-finite values.
Results may differ from a plain program's by a relative error of at most 0.0024.
Values may be sent and summed in bfloat16 or wider, within the bound.
A program may use at most 192 MiB of HBM per device.

v0:
```python
import functools

import jax
import jax.numpy as jnp
from jax import lax
from jax.experimental import pallas as pl
from jax.experimental.pallas import tpu as pltpu
from jax.sharding import PartitionSpec as P

BAND = 5
TERMS = 3
LANES = 128
CHUNK = 256
GROUP = 2


def kernel(
    n, col_hbm, ow_hbm, h_hbm, probe_hbm, prev_hbm, cur_hbm,
    tb, mom,
    col_ref, ow_ref, hv, hb, ext, wts, pv,
    in_sem, send_sem, recv_sem, msend, mrecv,
):
    me = lax.axis_index("slab")
    rows, slots, w, _ = hv.shape
    chunks, height, cc = wts.shape
    total = n * rows
    rim = BAND * w
    gw = GROUP * w
    pairs = rows // GROUP
    edge = -(-BAND // GROUP)
    depth = gw + 2 * rim
    first = me * rows
    far = lax.rem(me, 2)
    near = 1 - far

    def columns(c):
        return pl.ds(c * cc, cc)

    def rim_in(c, side):
        start = pl.multiple_of(side * (height - rim), w)
        return pltpu.make_async_copy(
            cur_hbm.at[pl.ds(start, rim), columns(c)],
            tb.at[1, c, pl.ds(start, rim)],
            in_sem.at[3 * c + side],
        )

    inner = height - 2 * rim
    inner_in = [
        pltpu.make_async_copy(
            cur_hbm.at[pl.ds(rim, inner), columns(c)], tb.at[1, c, pl.ds(rim, inner)],
            in_sem.at[3 * c + 2])
        for c in range(chunks)
    ]
    base = 3 * chunks
    h_in = pltpu.make_async_copy(h_hbm, hv, in_sem.at[base])
    probe_in = pltpu.make_async_copy(probe_hbm, pv, in_sem.at[base + 1])
    col_in = pltpu.make_async_copy(col_hbm, col_ref, in_sem.at[base + 2])
    ow_in = pltpu.make_async_copy(ow_hbm, ow_ref, in_sem.at[base + 3])
    prev_in = [
        pltpu.make_async_copy(prev_hbm.at[:, columns(c)], tb.at[0, c], in_sem.at[base + 4 + c])
        for c in range(chunks)
    ]
    for c in range(chunks):
        rim_in(c, far).start()
        rim_in(c, near).start()

    barrier = pltpu.get_barrier_semaphore()
    for k in range(1, n):
        pl.semaphore_signal(
            barrier, inc=1, device_id={"slab": lax.rem(me + k, n)},
            device_id_type=pl.DeviceIdType.MESH,
        )

    inside = BAND - GROUP

    def halo(t, c, side, part):
        size = (BAND - inside if part else inside) * w
        offset = (1 - side) * inside * w if part else side * (BAND - inside) * w
        source = pl.multiple_of(rim + side * (height - rim) + offset, w)
        target = pl.multiple_of((1 - side) * (rim + height) + offset, w)
        return pltpu.make_async_remote_copy(
            src_ref=ext.at[t, c, pl.ds(source, size)],
            dst_ref=ext.at[t, c, pl.ds(target, size)],
            send_sem=send_sem.at[t, c, side, part], recv_sem=recv_sem.at[t, c, 1 - side, part],
            device_id={"slab": lax.rem(me + n - 1 + 2 * side, n)},
            device_id_type=pl.DeviceIdType.MESH,
        )

    def cast(c, start, steps):
        def body(i, carry):
            at = pl.multiple_of(start + i * w, w)
            ext[0, c, pl.ds(pl.multiple_of(rim + at, w), w)] = tb[1, c, pl.ds(at, w)].astype(jnp.bfloat16)
            return carry

        lax.fori_loop(0, steps, body, 0)

    for c in range(chunks):
        for side in (far, near):
            rim_in(c, side).wait()
            cast(c, side * (height - rim), BAND)
            if c == 0 and side is far:
                for copy in inner_in:
                    copy.start()
                col_in.start()
                h_in.start()
                ow_in.start()
                probe_in.start()
                for copy in prev_in:
                    copy.start()
                pl.semaphore_wait(barrier, n - 1)
            for part in range(2):
                halo(0, c, side, part).start()
    for c in range(chunks):
        inner_in[c].wait()
        cast(c, rim, inner // w)

    col_in.wait()
    h_in.wait()
    zero = jnp.zeros((w, w), jnp.bfloat16)

    def build(p, carry):
        for half in range(GROUP):
            r = p * GROUP + half
            places = []
            for s in range(slots):
                x = col_ref[r, s] - (first + r) + BAND
                x = jnp.where(x < 0, x + total, x)
                places.append(jnp.where(x >= total, x - total, x))
            for d in range(GROUP + 2 * BAND):
                place = d - half
                if place < 0 or place > 2 * BAND:
                    block = zero
                else:
                    slot = jnp.int32(0)
                    hit = jnp.int32(0)
                    for s in range(slots):
                        same = places[s] == place
                        slot = jnp.where(same, s, slot)
                        hit = jnp.where(same, 1, hit)
                    block = jnp.where(hit == 1, hv[r, slot], zero)
                hb[p, half * w:(half + 1) * w, d * w:(d + 1) * w] = block
        return carry

    lax.fori_loop(0, pairs, build, 0)

    probe_in.wait()
    ow_in.wait()
    eye = lax.broadcasted_iota(jnp.int32, (w, w), 0) == lax.broadcasted_iota(jnp.int32, (w, w), 1)

    def weigh(r, carry):
        row = jnp.broadcast_to(ow_ref[pl.ds(r, 1), :], (w, w))
        column = jnp.sum(jnp.where(eye, row, 0.0), axis=1, keepdims=True) / (total * w)
        at = pl.multiple_of(r * w, w)
        for c in range(chunks):
            wts[c, pl.ds(at, w)] = column * pv[pl.ds(at, w), c * cc:(c + 1) * cc].astype(jnp.float32)
        return carry

    lax.fori_loop(0, rows, weigh, 0)
    for copy in prev_in:
        copy.wait()

    def tile(t, c, p, acc):
        at = pl.multiple_of(p * gw, gw)
        product = jnp.dot(hb[p], ext[t, c, pl.ds(at, depth)], preferred_element_type=jnp.float32)
        upcoming = 2.0 * product - tb[t % 2, c, pl.ds(at, gw)]
        tb[t % 2, c, pl.ds(at, gw)] = upcoming
        if t + 1 < TERMS:
            ext[t + 1, c, pl.ds(pl.multiple_of(rim + at, w), gw)] = upcoming.astype(jnp.bfloat16)
        y = wts[c, pl.ds(at, gw)] * upcoming
        return acc + jnp.sum(y.reshape(gw // 8, 8, cc), axis=0)

    def sums(t):
        return [
            pltpu.make_async_remote_copy(
                src_ref=mom.at[t, me], dst_ref=mom.at[t, me],
                send_sem=msend.at[t, k], recv_sem=mrecv.at[t, k],
                device_id={"slab": lax.rem(me + k, n)}, device_id_type=pl.DeviceIdType.MESH,
            )
            for k in range(1, n)
        ]

    sent = []
    for t in range(TERMS):
        for c in range(chunks):
            acc = jnp.zeros((8, cc), jnp.float32)
            acc = lax.fori_loop(edge, pairs - edge, lambda p, a: tile(t, c, p, a), acc)
            for side in (near, far):
                def rim_tile(i, a):
                    return tile(t, c, (1 - side) * (edge - 1 - i) + side * (pairs - edge + i), a)

                halo(t, c, 1 - side, 0).wait_recv()
                acc = lax.fori_loop(0, edge - 1, rim_tile, acc)
                halo(t, c, 1 - side, 1).wait_recv()
                acc = rim_tile(edge - 1, acc)
                if t + 1 < TERMS:
                    for part in range(2):
                        halo(t + 1, c, side, part).start()
            total_row = jnp.sum(acc, axis=0, keepdims=True)
            for k in range(cc // LANES):
                mom[t, me, pl.ds(c * (cc // LANES) + k, 1), :] = total_row[:, k * LANES:(k + 1) * LANES]
        copies = sums(t)
        for copy in copies:
            copy.start()
        sent.append(copies)

    for t in range(TERMS):
        for c in range(chunks):
            for side in (near, far):
                for part in range(2):
                    halo(t, c, side, part).wait_send()
    for copies in sent:
        for copy in copies:
            copy.wait()


def finish(tb, mom, last_prev, last_cur, mom_hbm, row_sums, sem):
    terms, n, lanes_of, _ = mom.shape
    _, chunks, _, cc = tb.shape
    copies = []
    for c in range(chunks):
        for k, out in enumerate((last_cur, last_prev)):
            source = (terms - 1 + k) % 2
            copies.append(pltpu.make_async_copy(
                tb.at[source, c], out.at[:, pl.ds(c * cc, cc)], sem.at[2 * c + k]))
    for copy in copies:
        copy.start()
    for t in range(terms):
        whole = mom[t, 0]
        for i in range(1, n):
            whole = whole + mom[t, i]
        for k in range(lanes_of):
            row_sums[t:t + 1, k * LANES:(k + 1) * LANES] = whole[k:k + 1, :]
    copies.append(pltpu.make_async_copy(row_sums, mom_hbm, sem.at[2 * chunks]))
    copies[-1].start()
    for copy in copies:
        copy.wait()


def local(hamiltonian_blocks, block_columns, probe, previous, current, orbital_weight):
    n = lax.axis_size("slab")
    rows, slots, w, _ = hamiltonian_blocks.shape
    height, cols = current.shape
    cc = min(CHUNK, cols)
    chunks = cols // cc
    vmem = pl.BlockSpec(memory_space=pltpu.VMEM)
    hbm = pl.BlockSpec(memory_space=pltpu.HBM)
    bf16, f32 = jnp.bfloat16, jnp.float32
    grant = 67043328 - 4 * (2 * height * cols + TERMS * n * cols) - (64 << 10)
    tb, mom = pl.pallas_call(
        functools.partial(kernel, n),
        out_shape=(
            pltpu.VMEM((2, chunks, height, cc), f32),
            pltpu.VMEM((TERMS, n, cols // LANES, LANES), f32),
        ),
        in_specs=[hbm] * 6,
        out_specs=(vmem, vmem),
        scratch_shapes=[
            pltpu.SMEM((rows, slots), jnp.int32),
            pltpu.VMEM((rows, w), f32),
            pltpu.VMEM((rows, slots, w, w), bf16),
            pltpu.VMEM((rows // GROUP, GROUP * w, (GROUP + 2 * BAND) * w), bf16),
            pltpu.VMEM((TERMS, chunks, height + 2 * BAND * w, cc), bf16),
            pltpu.VMEM((chunks, height, cc), f32),
            pltpu.VMEM((height, cols), bf16),
            pltpu.SemaphoreType.DMA((4 * chunks + 4,)),
            pltpu.SemaphoreType.DMA((TERMS, chunks, 2, 2)),
            pltpu.SemaphoreType.DMA((TERMS, chunks, 2, 2)),
            pltpu.SemaphoreType.DMA((TERMS, n)),
            pltpu.SemaphoreType.DMA((TERMS, n)),
        ],
        compiler_params=pltpu.CompilerParams(
            collective_id=0, has_side_effects=True, vmem_limit_bytes=grant,
        ),
    )(block_columns, orbital_weight.reshape(rows, w), hamiltonian_blocks, probe, previous, current)
    return pl.pallas_call(
        finish,
        out_shape=(
            jax.ShapeDtypeStruct((height, cols), f32),
            jax.ShapeDtypeStruct((height, cols), f32),
            jax.ShapeDtypeStruct((TERMS, cols), f32),
        ),
        in_specs=[vmem, vmem],
        out_specs=(hbm, hbm, hbm),
        scratch_shapes=[
            pltpu.VMEM((TERMS, cols), f32),
            pltpu.SemaphoreType.DMA((2 * chunks + 1,)),
        ],
        compiler_params=pltpu.CompilerParams(vmem_limit_bytes=16 * 1024 * 1024),
    )(tb, mom)


def solution(mesh):
    return jax.shard_map(
        local,
        mesh=mesh,
        in_specs=(
            P("slab", None, None, None),
            P("slab", None),
            P("slab", "col"),
            P("slab", "col"),
            P("slab", "col"),
            P("slab"),
        ),
        out_specs=(P("slab", "col"), P("slab", "col"), P(None, "col")),
        check_vma=False,
    )
```

profile of v0, /device:TPU:0, one launch (start us, length us, event | category | flops | bytes accessed | tf_op | source)
XLA Modules:
  0.0 56.3 jit_solution(5583989961487576398)
XLA Ops:
  0.6 52.3 %shard_map.85 = (f32[2,2,2048,256]{3,2,1,0:T(8,128)S(1)}, f32[3,8,4,128]{3,2,1,0:T(4,128)S(1)}) custom-call(s32[16,9]{1,0:T(8,128)} %col_hbm.1, f32[16,128]{1,0:T(8,128)} %bitcast.1, bf16[16,9,128,128]{3,2,1,0:T(8,128)(2,1)} %h_hbm.1, bf16[2048,512]{1,0:T(8,128)(2,1)} %probe_hbm.1, f32[2048,512]{1,0:T(8,128)} %prev_hbm.1, f32[2048,512]{1,0:T(8,128)} %cur_hbm.1), custom_call_target="tpu_custom_call" | custom-call | tf_op jit(solution)/shard_map/pallas_call | solution.py:249
  53.0 3.4 %shard_map.86 = (f32[2048,512]{1,0:T(8,128)}, f32[2048,512]{1,0:T(8,128)}, f32[3,512]{1,0:T(4,128)}) custom-call(f32[2,2,2048,256]{3,2,1,0:T(8,128)S(1)} %get-tuple-element.5.tb, f32[3,8,4,128]{3,2,1,0:T(4,128)S(1)} %get-tuple-element.6.mom), custom_call_target="tpu_custom_call" | custom-call | tf_op jit(solution)/shard_map/pallas_call | solution.py:275
where the time goes:
time: 56.5 us; the launch traced here: 56.3 us
  Pallas kernels  55.7 us (99%)
  between operations  0.64 us (1%)
    pallas_call x1, Pallas kernels, local(): pl.pallas_call(functools.partial(kernel, n), out_shape=(pltpu.VMEM((2, ch...  52.3 us
    pallas_call x1, Pallas kernels, local(): pl.pallas_call(finish, out_shape=(jax.ShapeDtypeStruct((height, cols), f3...  3.38 us

commit v1 on v0

--- a/solution.py
+++ b/solution.py
@@ -18,7 +18,7 @@
     n, col_hbm, ow_hbm, h_hbm, probe_hbm, prev_hbm, cur_hbm,
     tb, mom,
     col_ref, ow_ref, hv, hb, ext, wts, pv,
-    in_sem, send_sem, recv_sem, msend, mrecv,
+    in_sem, send_sem, recv_sem, msend, mrecv, known,
 ):
     me = lax.axis_index("slab")
     rows, slots, w, _ = hv.shape
@@ -36,12 +36,22 @@
     def columns(c):
         return pl.ds(c * cc, cc)
 
-    def rim_in(c, side):
-        start = pl.multiple_of(side * (height - rim), w)
+    inside = BAND - GROUP
+    parts = ((0, inside), (inside, BAND))
+
+    def layers(side, a, b):
+        return (1 - side) * a * w + side * (BAND - b) * w
+
+    def pieces(c, side):
+        return ((0, 1), (1, inside), (inside, BAND)) if c == 0 and side is far else ((0, BAND),)
+
+    def rim_in(c, side, k):
+        a, b = pieces(c, side)[k]
+        start = pl.multiple_of(side * (height - rim) + layers(side, a, b), w)
         return pltpu.make_async_copy(
-            cur_hbm.at[pl.ds(start, rim), columns(c)],
-            tb.at[1, c, pl.ds(start, rim)],
-            in_sem.at[3 * c + side],
+            cur_hbm.at[pl.ds(start, (b - a) * w), columns(c)],
+            tb.at[1, c, pl.ds(start, (b - a) * w)],
+            in_sem.at[3 * c + side] if k == 0 else in_sem.at[3 * chunks + 3 + chunks + k],
         )
 
     inner = height - 2 * rim
@@ -60,28 +70,32 @@
         pltpu.make_async_copy(prev_hbm.at[:, columns(c)], tb.at[0, c], in_sem.at[base + 4 + c])
         for c in range(chunks)
     ]
+    barrier = pltpu.get_barrier_semaphore()
+
+    def greet(semaphore, distance):
+        for other in (n - distance, distance):
+            pl.semaphore_signal(
+                semaphore, inc=1, device_id={"slab": lax.rem(me + other, n)},
+                device_id_type=pl.DeviceIdType.MESH,
+            )
+
+    greet(barrier, 1)
     for c in range(chunks):
-        rim_in(c, far).start()
-        rim_in(c, near).start()
-
-    barrier = pltpu.get_barrier_semaphore()
-    for k in range(1, n):
-        pl.semaphore_signal(
-            barrier, inc=1, device_id={"slab": lax.rem(me + k, n)},
-            device_id_type=pl.DeviceIdType.MESH,
-        )
-
-    inside = BAND - GROUP
-
-    def halo(t, c, side, part):
-        size = (BAND - inside if part else inside) * w
-        offset = (1 - side) * inside * w if part else side * (BAND - inside) * w
+        for side in (far, near):
+            for k in range(len(pieces(c, side))):
+                rim_in(c, side, k).start()
+
+    def halo(t, c, side, part, a=None, b=None):
+        if a is None:
+            a, b = parts[part]
+        size = (b - a) * w
+        offset = layers(side, a, b)
         source = pl.multiple_of(rim + side * (height - rim) + offset, w)
         target = pl.multiple_of((1 - side) * (rim + height) + offset, w)
         return pltpu.make_async_remote_copy(
             src_ref=ext.at[t, c, pl.ds(source, size)],
             dst_ref=ext.at[t, c, pl.ds(target, size)],
-            send_sem=send_sem.at[t, c, side, part], recv_sem=recv_sem.at[t, c, 1 - side, part],
+            send_sem=send_sem, recv_sem=recv_sem.at[t, c, 1 - side, part],
             device_id={"slab": lax.rem(me + n - 1 + 2 * side, n)},
             device_id_type=pl.DeviceIdType.MESH,
         )
@@ -94,10 +108,18 @@
 
         lax.fori_loop(0, steps, body, 0)
 
+    rounds = known.shape[0]
     for c in range(chunks):
         for side in (far, near):
-            rim_in(c, side).wait()
-            cast(c, side * (height - rim), BAND)
+            for k, (a, b) in enumerate(pieces(c, side)):
+                rim_in(c, side, k).wait()
+                cast(c, side * (height - rim) + layers(side, a, b), b - a)
+                if c == 0 and side is far and k == 0:
+                    pl.semaphore_wait(barrier, 2)
+                for part, (low, high) in enumerate(parts):
+                    low, high = max(low, a), min(high, b)
+                    if low < high:
+                        halo(0, c, side, part, low, high).start()
             if c == 0 and side is far:
                 for copy in inner_in:
                     copy.start()
@@ -107,9 +129,7 @@
                 probe_in.start()
                 for copy in prev_in:
                     copy.start()
-                pl.semaphore_wait(barrier, n - 1)
-            for part in range(2):
-                halo(0, c, side, part).start()
+                greet(known.at[0], 1)
     for c in range(chunks):
         inner_in[c].wait()
         cast(c, rim, inner // w)
@@ -169,17 +189,19 @@
         y = wts[c, pl.ds(at, gw)] * upcoming
         return acc + jnp.sum(y.reshape(gw // 8, 8, cc), axis=0)
 
-    def sums(t):
-        return [
-            pltpu.make_async_remote_copy(
-                src_ref=mom.at[t, me], dst_ref=mom.at[t, me],
-                send_sem=msend.at[t, k], recv_sem=mrecv.at[t, k],
-                device_id={"slab": lax.rem(me + k, n)}, device_id_type=pl.DeviceIdType.MESH,
-            )
-            for k in range(1, n)
-        ]
-
-    sent = []
+    def moments(t, k, rest=None):
+        block = mom.at[t, me] if rest is None else rest
+        return pltpu.make_async_remote_copy(
+            src_ref=block, dst_ref=block, send_sem=msend, recv_sem=mrecv.at[t],
+            device_id={"slab": lax.rem(me + k, n)}, device_id_type=pl.DeviceIdType.MESH,
+        )
+
+    def spread(start, stop):
+        for k in range(start, stop):
+            pl.semaphore_wait(known.at[k], 2)
+            if k + 1 < rounds:
+                greet(known.at[k + 1], 2 ** (k + 1))
+
     for t in range(TERMS):
         for c in range(chunks):
             acc = jnp.zeros((8, cc), jnp.float32)
@@ -198,19 +220,20 @@
             total_row = jnp.sum(acc, axis=0, keepdims=True)
             for k in range(cc // LANES):
                 mom[t, me, pl.ds(c * (cc // LANES) + k, 1), :] = total_row[:, k * LANES:(k + 1) * LANES]
-        copies = sums(t)
-        for copy in copies:
-            copy.start()
-        sent.append(copies)
-
+            if t == 0:
+                spread(0 if c == 0 else 1, 1 if c + 1 < chunks else rounds)
+        for k in range(1, n):
+            moments(t, k).start()
+
+    pltpu.make_async_remote_copy(
+        src_ref=ext.at[:, :, pl.ds(0, 2 * rim)], dst_ref=ext.at[:, :, pl.ds(0, 2 * rim)],
+        send_sem=send_sem, recv_sem=msend, device_id={"slab": lax.rem(me + 1, n)},
+        device_id_type=pl.DeviceIdType.MESH,
+    ).wait_send()
+    others = mom.at[:, pl.ds(0, n - 1)]
+    moments(0, 1, others).wait_send()
     for t in range(TERMS):
-        for c in range(chunks):
-            for side in (near, far):
-                for part in range(2):
-                    halo(t, c, side, part).wait_send()
-    for copies in sent:
-        for copy in copies:
-            copy.wait()
+        moments(t, 1, mom.at[t, pl.ds(0, n - 1)]).wait_recv()
 
 
 def finish(tb, mom, last_prev, last_cur, mom_hbm, row_sums, sem):
@@ -262,11 +285,12 @@
             pltpu.VMEM((TERMS, chunks, height + 2 * BAND * w, cc), bf16),
             pltpu.VMEM((chunks, height, cc), f32),
             pltpu.VMEM((height, cols), bf16),
-            pltpu.SemaphoreType.DMA((4 * chunks + 4,)),
+            pltpu.SemaphoreType.DMA((4 * chunks + 6,)),
+            pltpu.SemaphoreType.DMA,
             pltpu.SemaphoreType.DMA((TERMS, chunks, 2, 2)),
-            pltpu.SemaphoreType.DMA((TERMS, chunks, 2, 2)),
-            pltpu.SemaphoreType.DMA((TERMS, n)),
-            pltpu.SemaphoreType.DMA((TERMS, n)),
+            pltpu.SemaphoreType.DMA,
+            pltpu.SemaphoreType.DMA((TERMS,)),
+            pltpu.SemaphoreType.REGULAR((max(1, (n // 2 - 1).bit_length()),)),
         ],
         compiler_params=pltpu.CompilerParams(
             collective_id=0, has_side_effects=True, vmem_limit_bytes=grant,

time: 56.5 us -> 55.8 us (0.988)
  Pallas kernels: 55.7 us -> 55 us
    pallas_call x1, Pallas kernels: 52.3 us -> 51.6 us  [local(): pl.pallas_call(functools.partial(kernel, n), out_shape=(pltpu.VMEM((2, ch...]
where the time goes in v1:
time: 55.8 us; the launch traced here: 55.6 us
  Pallas kernels  55 us (99%)
  between operations  0.64 us (1%)
    pallas_call x1, Pallas kernels, local(): pl.pallas_call(functools.partial(kernel, n), out_shape=(pltpu.VMEM((2, ch...  51.6 us
    pallas_call x1, Pallas kernels, local(): pl.pallas_call(finish, out_shape=(jax.ShapeDtypeStruct((height, cols), f3...  3.38 us

profile of v1, /device:TPU:0, one launch (start us, length us, event | category | flops | bytes accessed | tf_op | source)
XLA Modules:
  0.0 55.6 jit_solution(3779068915640965744)
XLA Ops:
  0.6 51.6 %shard_map.85 = (f32[2,2,2048,256]{3,2,1,0:T(8,128)S(1)}, f32[3,8,4,128]{3,2,1,0:T(4,128)S(1)}) custom-call(s32[16,9]{1,0:T(8,128)} %col_hbm.1, f32[16,128]{1,0:T(8,128)} %bitcast.1, bf16[16,9,128,128]{3,2,1,0:T(8,128)(2,1)} %h_hbm.1, bf16[2048,512]{1,0:T(8,128)(2,1)} %probe_hbm.1, f32[2048,512]{1,0:T(8,128)} %prev_hbm.1, f32[2048,512]{1,0:T(8,128)} %cur_hbm.1), custom_call_target="tpu_custom_call" | custom-call | tf_op jit(solution)/shard_map/pallas_call | solution.py:272
  52.3 3.4 %shard_map.86 = (f32[2048,512]{1,0:T(8,128)}, f32[2048,512]{1,0:T(8,128)}, f32[3,512]{1,0:T(4,128)}) custom-call(f32[2,2,2048,256]{3,2,1,0:T(8,128)S(1)} %get-tuple-element.5.tb, f32[3,8,4,128]{3,2,1,0:T(4,128)S(1)} %get-tuple-element.6.mom), custom_call_target="tpu_custom_call" | custom-call | tf_op jit(solution)/shard_map/pallas_call | solution.py:299

commit v2 on v1

--- a/solution.py
+++ b/solution.py
@@ -12,13 +12,14 @@
 LANES = 128
 CHUNK = 256
 GROUP = 2
+LEAD = 3
 
 
 def kernel(
     n, col_hbm, ow_hbm, h_hbm, probe_hbm, prev_hbm, cur_hbm,
     tb, mom,
     col_ref, ow_ref, hv, hb, ext, wts, pv,
-    in_sem, send_sem, recv_sem, msend, mrecv, known,
+    in_sem, send_sem, recv_sem, msend, mrecv, known, gate_sem, turn,
 ):
     me = lax.axis_index("slab")
     rows, slots, w, _ = hv.shape
@@ -51,23 +52,22 @@
         return pltpu.make_async_copy(
             cur_hbm.at[pl.ds(start, (b - a) * w), columns(c)],
             tb.at[1, c, pl.ds(start, (b - a) * w)],
-            in_sem.at[3 * c + side] if k == 0 else in_sem.at[3 * chunks + 3 + chunks + k],
+            in_sem.at[6 + (k if c == 0 and side is far else 2 * c + (2 if side is far else 3))],
         )
 
     inner = height - 2 * rim
     inner_in = [
         pltpu.make_async_copy(
             cur_hbm.at[pl.ds(rim, inner), columns(c)], tb.at[1, c, pl.ds(rim, inner)],
-            in_sem.at[3 * c + 2])
+            in_sem.at[0])
         for c in range(chunks)
     ]
-    base = 3 * chunks
-    h_in = pltpu.make_async_copy(h_hbm, hv, in_sem.at[base])
-    probe_in = pltpu.make_async_copy(probe_hbm, pv, in_sem.at[base + 1])
-    col_in = pltpu.make_async_copy(col_hbm, col_ref, in_sem.at[base + 2])
-    ow_in = pltpu.make_async_copy(ow_hbm, ow_ref, in_sem.at[base + 3])
+    h_in = pltpu.make_async_copy(h_hbm, hv, in_sem.at[1])
+    probe_in = pltpu.make_async_copy(probe_hbm, pv, in_sem.at[2])
+    col_in = pltpu.make_async_copy(col_hbm, col_ref, in_sem.at[3])
+    ow_in = pltpu.make_async_copy(ow_hbm, ow_ref, in_sem.at[4])
     prev_in = [
-        pltpu.make_async_copy(prev_hbm.at[:, columns(c)], tb.at[0, c], in_sem.at[base + 4 + c])
+        pltpu.make_async_copy(prev_hbm.at[:, columns(c)], tb.at[0, c], in_sem.at[5])
         for c in range(chunks)
     ]
     barrier = pltpu.get_barrier_semaphore()
@@ -85,7 +85,16 @@
             for k in range(len(pieces(c, side))):
                 rim_in(c, side, k).start()
 
-    def halo(t, c, side, part, a=None, b=None):
+    def hops(chip):
+        return lax.rem(chip, 2) + lax.rem(chip // 2, 2)
+
+    chip = me // 2
+    every = n // 2
+    mine = hops(lax.rem(chip + every - 1 + 2 * far, every))
+    other = hops(lax.rem(chip + every - 1 + 2 * near, every))
+    last = (TERMS - 1, chunks - 1)
+
+    def halo(t, c, side, part, a=None, b=None, gate=None):
         if a is None:
             a, b = parts[part]
         size = (b - a) * w
@@ -95,7 +104,8 @@
         return pltpu.make_async_remote_copy(
             src_ref=ext.at[t, c, pl.ds(source, size)],
             dst_ref=ext.at[t, c, pl.ds(target, size)],
-            send_sem=send_sem, recv_sem=recv_sem.at[t, c, 1 - side, part],
+            send_sem=send_sem if gate is None else gate,
+            recv_sem=recv_sem.at[t % 2, c, 1 - side, part],
             device_id={"slab": lax.rem(me + n - 1 + 2 * side, n)},
             device_id_type=pl.DeviceIdType.MESH,
         )
@@ -130,8 +140,9 @@
                 for copy in prev_in:
                     copy.start()
                 greet(known.at[0], 1)
-    for c in range(chunks):
-        inner_in[c].wait()
+    inside_of = tb.at[1, :, pl.ds(rim, inner)]
+    pltpu.make_async_copy(inside_of, inside_of, in_sem.at[0]).wait()
+    for c in range(chunks):
         cast(c, rim, inner // w)
 
     col_in.wait()
@@ -176,8 +187,7 @@
         return carry
 
     lax.fori_loop(0, rows, weigh, 0)
-    for copy in prev_in:
-        copy.wait()
+    pltpu.make_async_copy(tb.at[0], tb.at[0], in_sem.at[5]).wait()
 
     def tile(t, c, p, acc):
         at = pl.multiple_of(p * gw, gw)
@@ -189,10 +199,11 @@
         y = wts[c, pl.ds(at, gw)] * upcoming
         return acc + jnp.sum(y.reshape(gw // 8, 8, cc), axis=0)
 
-    def moments(t, k, rest=None):
-        block = mom.at[t, me] if rest is None else rest
+    def moments(final, k, first=me, count=1):
+        terms = pl.ds(TERMS - 1, 1) if final else pl.ds(0, TERMS - 1)
+        block = mom.at[pl.ds(first, count), terms]
         return pltpu.make_async_remote_copy(
-            src_ref=block, dst_ref=block, send_sem=msend, recv_sem=mrecv.at[t],
+            src_ref=block, dst_ref=block, send_sem=msend, recv_sem=mrecv.at[final],
             device_id={"slab": lax.rem(me + k, n)}, device_id_type=pl.DeviceIdType.MESH,
         )
 
@@ -210,34 +221,59 @@
                 def rim_tile(i, a):
                     return tile(t, c, (1 - side) * (edge - 1 - i) + side * (pairs - edge + i), a)
 
+                if (t, c) == last and side is far:
+                    halo(t, c, side, 0, 0, LEAD, gate_sem).wait_send()
+
+                    @pl.when(mine > other)
+                    def _():
+                        pl.semaphore_signal(
+                            turn, inc=1, device_id={"slab": lax.rem(me + n - 1 + 2 * near, n)},
+                            device_id_type=pl.DeviceIdType.MESH)
+
+                    @pl.when(mine < other)
+                    def _():
+                        pl.semaphore_wait(turn, 1)
+                        halo(t, c, side, 1).start()
+
                 halo(t, c, 1 - side, 0).wait_recv()
                 acc = lax.fori_loop(0, edge - 1, rim_tile, acc)
                 halo(t, c, 1 - side, 1).wait_recv()
+                if (t, c) == last and side is far:
+                    for k in range(1, n):
+                        moments(0, k).start()
                 acc = rim_tile(edge - 1, acc)
                 if t + 1 < TERMS:
-                    for part in range(2):
-                        halo(t + 1, c, side, part).start()
+                    if (t + 1, c) == last and side is far:
+                        halo(t + 1, c, side, 0, 0, LEAD, gate_sem).start()
+                        if LEAD < inside:
+                            halo(t + 1, c, side, 0, LEAD, inside).start()
+                        pl.when(mine >= other)(halo(t + 1, c, side, 1).start)
+                    else:
+                        for part in range(2):
+                            halo(t + 1, c, side, part).start()
             total_row = jnp.sum(acc, axis=0, keepdims=True)
             for k in range(cc // LANES):
-                mom[t, me, pl.ds(c * (cc // LANES) + k, 1), :] = total_row[:, k * LANES:(k + 1) * LANES]
+                mom[me, t, pl.ds(c * (cc // LANES) + k, 1), :] = total_row[:, k * LANES:(k + 1) * LANES]
             if t == 0:
                 spread(0 if c == 0 else 1, 1 if c + 1 < chunks else rounds)
-        for k in range(1, n):
-            moments(t, k).start()
+    for k in range(1, n):
+        moments(1, k).start()
 
     pltpu.make_async_remote_copy(
-        src_ref=ext.at[:, :, pl.ds(0, 2 * rim)], dst_ref=ext.at[:, :, pl.ds(0, 2 * rim)],
+        src_ref=ext.at[0:TERMS - 1, :, pl.ds(0, 2 * rim)], dst_ref=ext.at[0:TERMS - 1, :, pl.ds(0, 2 * rim)],
         send_sem=send_sem, recv_sem=msend, device_id={"slab": lax.rem(me + 1, n)},
         device_id_type=pl.DeviceIdType.MESH,
     ).wait_send()
-    others = mom.at[:, pl.ds(0, n - 1)]
-    moments(0, 1, others).wait_send()
-    for t in range(TERMS):
-        moments(t, 1, mom.at[t, pl.ds(0, n - 1)]).wait_recv()
+    for c in range(chunks):
+        for side in (near, far):
+            held = LEAD if (TERMS - 1, c) == last and side is far else 0
+            halo(TERMS - 1, c, side, 0, held, BAND).wait_send()
+    for final in range(2):
+        moments(final, 1, 0, n - 1).wait()
 
 
 def finish(tb, mom, last_prev, last_cur, mom_hbm, row_sums, sem):
-    terms, n, lanes_of, _ = mom.shape
+    n, terms, lanes_of, _ = mom.shape
     _, chunks, _, cc = tb.shape
     copies = []
     for c in range(chunks):
@@ -248,9 +284,9 @@
     for copy in copies:
         copy.start()
     for t in range(terms):
-        whole = mom[t, 0]
+        whole = mom[0, t]
         for i in range(1, n):
-            whole = whole + mom[t, i]
+            whole = whole + mom[i, t]
         for k in range(lanes_of):
             row_sums[t:t + 1, k * LANES:(k + 1) * LANES] = whole[k:k + 1, :]
     copies.append(pltpu.make_async_copy(row_sums, mom_hbm, sem.at[2 * chunks]))
@@ -273,7 +309,7 @@
         functools.partial(kernel, n),
         out_shape=(
             pltpu.VMEM((2, chunks, height, cc), f32),
-            pltpu.VMEM((TERMS, n, cols // LANES, LANES), f32),
+            pltpu.VMEM((n, TERMS, cols // LANES, LANES), f32),
         ),
         in_specs=[hbm] * 6,
         out_specs=(vmem, vmem),
@@ -285,12 +321,14 @@
             pltpu.VMEM((TERMS, chunks, height + 2 * BAND * w, cc), bf16),
             pltpu.VMEM((chunks, height, cc), f32),
             pltpu.VMEM((height, cols), bf16),
-            pltpu.SemaphoreType.DMA((4 * chunks + 6,)),
+            pltpu.SemaphoreType.DMA((8 + 2 * chunks,)),
             pltpu.SemaphoreType.DMA,
-            pltpu.SemaphoreType.DMA((TERMS, chunks, 2, 2)),
+            pltpu.SemaphoreType.DMA((2, chunks, 2, 2)),
             pltpu.SemaphoreType.DMA,
-            pltpu.SemaphoreType.DMA((TERMS,)),
+            pltpu.SemaphoreType.DMA((2,)),
             pltpu.SemaphoreType.REGULAR((max(1, (n // 2 - 1).bit_length()),)),
+            pltpu.SemaphoreType.DMA,
+            pltpu.SemaphoreType.REGULAR,
         ],
         compiler_params=pltpu.CompilerParams(
             collective_id=0, has_side_effects=True, vmem_limit_bytes=grant,

time: 55.8 us -> 54.7 us (0.980)
  Pallas kernels: 55 us -> 53.9 us
    pallas_call x1, Pallas kernels: 51.6 us -> 50.5 us  [local(): pl.pallas_call(functools.partial(kernel, n), out_shape=(pltpu.VMEM((2, ch...]
where the time goes in v2:
time: 54.7 us; the launch traced here: 54.5 us
  Pallas kernels  53.9 us (99%)
  between operations  0.64 us (1%)
    pallas_call x1, Pallas kernels, local(): pl.pallas_call(functools.partial(kernel, n), out_shape=(pltpu.VMEM((2, ch...  50.5 us
    pallas_call x1, Pallas kernels, local(): pl.pallas_call(finish, out_shape=(jax.ShapeDtypeStruct((height, cols), f3...  3.38 us

profile of v2, /device:TPU:0, one launch (start us, length us, event | category | flops | bytes accessed | tf_op | source)
XLA Modules:
  0.0 54.5 jit_solution(4079148656410998682)
XLA Ops:
  0.6 50.5 %shard_map.85 = (f32[2,2,2048,256]{3,2,1,0:T(8,128)S(1)}, f32[8,3,4,128]{3,2,1,0:T(4,128)S(1)}) custom-call(s32[16,9]{1,0:T(8,128)} %col_hbm.1, f32[16,128]{1,0:T(8,128)} %bitcast.1, bf16[16,9,128,128]{3,2,1,0:T(8,128)(2,1)} %h_hbm.1, bf16[2048,512]{1,0:T(8,128)(2,1)} %probe_hbm.1, f32[2048,512]{1,0:T(8,128)} %prev_hbm.1, f32[2048,512]{1,0:T(8,128)} %cur_hbm.1), custom_call_target="tpu_custom_call" | custom-call | tf_op jit(solution)/shard_map/pallas_call | solution.py:308
  51.2 3.4 %shard_map.86 = (f32[2048,512]{1,0:T(8,128)}, f32[2048,512]{1,0:T(8,128)}, f32[3,512]{1,0:T(4,128)}) custom-call(f32[2,2,2048,256]{3,2,1,0:T(8,128)S(1)} %get-tuple-element.5.tb, f32[8,3,4,128]{3,2,1,0:T(4,128)S(1)} %get-tuple-element.6.mom), custom_call_target="tpu_custom_call" | custom-call | tf_op jit(solution)/shard_map/pallas_call | solution.py:337

commit v3 on v2

--- a/solution.py
+++ b/solution.py
@@ -12,12 +12,11 @@
 LANES = 128
 CHUNK = 256
 GROUP = 2
-LEAD = 3
 
 
 def kernel(
     n, col_hbm, ow_hbm, h_hbm, probe_hbm, prev_hbm, cur_hbm,
-    tb, mom,
+    tb, mom, duo,
     col_ref, ow_ref, hv, hb, ext, wts, pv,
     in_sem, send_sem, recv_sem, msend, mrecv, known, gate_sem, turn,
 ):
@@ -37,22 +36,26 @@
     def columns(c):
         return pl.ds(c * cc, cc)
 
-    inside = BAND - GROUP
-    parts = ((0, inside), (inside, BAND))
-
-    def layers(side, a, b):
-        return (1 - side) * a * w + side * (BAND - b) * w
+    inside = (BAND - GROUP) * w
+    opening = (0, w // 8, 3 * w // 8, w, inside, rim)
+
+    def parts(side):
+        return ((0, inside), (inside, rim)) if side is far else ((0, rim),)
+
+    def from_edge(side, a, b):
+        return (1 - side) * a + side * (rim - b)
 
     def pieces(c, side):
-        return ((0, 1), (1, inside), (inside, BAND)) if c == 0 and side is far else ((0, BAND),)
+        return tuple(zip(opening, opening[1:])) if c == 0 and side is far else ((0, rim),)
 
     def rim_in(c, side, k):
         a, b = pieces(c, side)[k]
-        start = pl.multiple_of(side * (height - rim) + layers(side, a, b), w)
+        start = pl.multiple_of(side * (height - rim) + from_edge(side, a, b), w // 8)
+        spot = k if c == 0 and side is far else len(opening) - 2 + 2 * c + (0 if side is far else 1)
         return pltpu.make_async_copy(
-            cur_hbm.at[pl.ds(start, (b - a) * w), columns(c)],
-            tb.at[1, c, pl.ds(start, (b - a) * w)],
-            in_sem.at[6 + (k if c == 0 and side is far else 2 * c + (2 if side is far else 3))],
+            cur_hbm.at[pl.ds(start, b - a), columns(c)],
+            tb.at[1, c, pl.ds(start, b - a)],
+            in_sem.at[6 + spot],
         )
 
     inner = height - 2 * rim
@@ -96,37 +99,50 @@
 
     def halo(t, c, side, part, a=None, b=None, gate=None):
         if a is None:
-            a, b = parts[part]
-        size = (b - a) * w
-        offset = layers(side, a, b)
-        source = pl.multiple_of(rim + side * (height - rim) + offset, w)
-        target = pl.multiple_of((1 - side) * (rim + height) + offset, w)
+            a, b = parts(side)[part]
+        size = b - a
+        offset = from_edge(side, a, b)
+        source = pl.multiple_of(rim + side * (height - rim) + offset, w // 8)
+        target = pl.multiple_of((1 - side) * (rim + height) + offset, w // 8)
         return pltpu.make_async_remote_copy(
             src_ref=ext.at[t, c, pl.ds(source, size)],
             dst_ref=ext.at[t, c, pl.ds(target, size)],
             send_sem=send_sem if gate is None else gate,
-            recv_sem=recv_sem.at[t % 2, c, 1 - side, part],
+            recv_sem=recv_sem.at[t % 2, c, 1 + part if side is far else 0],
             device_id={"slab": lax.rem(me + n - 1 + 2 * side, n)},
             device_id_type=pl.DeviceIdType.MESH,
         )
 
-    def cast(c, start, steps):
+    def arrival(t, c, side, part):
+        a, b = parts(side)[part]
+        start = pl.multiple_of(side * (rim + height) + (1 - side) * (rim - b) + side * a, w // 8)
+        landed = ext.at[t, c, pl.ds(start, b - a)]
+        return pltpu.make_async_remote_copy(
+            src_ref=landed, dst_ref=landed, send_sem=send_sem,
+            recv_sem=recv_sem.at[t % 2, c, 1 + part if side is far else 0],
+            device_id={"slab": lax.rem(me + n - 1 + 2 * side, n)},
+            device_id_type=pl.DeviceIdType.MESH,
+        )
+
+    def cast(c, start, size):
+        step = min(size, w)
+
         def body(i, carry):
-            at = pl.multiple_of(start + i * w, w)
-            ext[0, c, pl.ds(pl.multiple_of(rim + at, w), w)] = tb[1, c, pl.ds(at, w)].astype(jnp.bfloat16)
+            at = pl.multiple_of(start + i * step, w // 8)
+            ext[0, c, pl.ds(pl.multiple_of(rim + at, w // 8), step)] = tb[1, c, pl.ds(at, step)].astype(jnp.bfloat16)
             return carry
 
-        lax.fori_loop(0, steps, body, 0)
+        lax.fori_loop(0, size // step, body, 0)
 
     rounds = known.shape[0]
     for c in range(chunks):
         for side in (far, near):
             for k, (a, b) in enumerate(pieces(c, side)):
                 rim_in(c, side, k).wait()
-                cast(c, side * (height - rim) + layers(side, a, b), b - a)
+                cast(c, side * (height - rim) + from_edge(side, a, b), b - a)
                 if c == 0 and side is far and k == 0:
                     pl.semaphore_wait(barrier, 2)
-                for part, (low, high) in enumerate(parts):
+                for part, (low, high) in enumerate(parts(side)):
                     low, high = max(low, a), min(high, b)
                     if low < high:
                         halo(0, c, side, part, low, high).start()
@@ -143,7 +159,7 @@
     inside_of = tb.at[1, :, pl.ds(rim, inner)]
     pltpu.make_async_copy(inside_of, inside_of, in_sem.at[0]).wait()
     for c in range(chunks):
-        cast(c, rim, inner // w)
+        cast(c, rim, inner)
 
     col_in.wait()
     h_in.wait()
@@ -199,13 +215,39 @@
         y = wts[c, pl.ds(at, gw)] * upcoming
         return acc + jnp.sum(y.reshape(gw // 8, 8, cc), axis=0)
 
-    def moments(final, k, first=me, count=1):
-        terms = pl.ds(TERMS - 1, 1) if final else pl.ds(0, TERMS - 1)
-        block = mom.at[pl.ds(first, count), terms]
+    late = rim - inside
+
+    def split_tile(t, c, side, acc):
+        p = side * (pairs - 1)
+        at = pl.multiple_of(p * gw, gw)
+        rows_of = pl.ds(at, gw)
+
+        def twice(offset, size):
+            offset = pl.multiple_of(offset, w)
+            return 2.0 * jnp.dot(
+                hb[p, :, pl.ds(offset, size)], ext[t, c, pl.ds(pl.multiple_of(at + offset, w), size)],
+                preferred_element_type=jnp.float32)
+
+        def weighed(value):
+            return jnp.sum((wts[c, rows_of] * value).reshape(gw // 8, 8, cc), axis=0)
+
+        begun = twice((1 - side) * late, depth - late) - tb[t % 2, c, rows_of]
+        tb[t % 2, c, rows_of] = begun
+        acc = acc + weighed(begun)
+        arrival(t, c, side, 1).wait_recv()
+        rest = twice(side * (depth - late), late)
+        tb[t % 2, c, rows_of] = tb[t % 2, c, rows_of] + rest
+        return acc + weighed(rest)
+
+    def to(block, k, semaphore):
         return pltpu.make_async_remote_copy(
-            src_ref=block, dst_ref=block, send_sem=msend, recv_sem=mrecv.at[final],
+            src_ref=block, dst_ref=block, send_sem=msend, recv_sem=mrecv.at[semaphore],
             device_id={"slab": lax.rem(me + k, n)}, device_id_type=pl.DeviceIdType.MESH,
         )
+
+    partner = n - 1 + 2 * near
+    early = pl.ds(0, TERMS - 1)
+    pair = to(mom.at[me, early], partner, 2)
 
     def spread(start, stop):
         for k in range(start, stop):
@@ -222,7 +264,7 @@
                     return tile(t, c, (1 - side) * (edge - 1 - i) + side * (pairs - edge + i), a)
 
                 if (t, c) == last and side is far:
-                    halo(t, c, side, 0, 0, LEAD, gate_sem).wait_send()
+                    halo(t, c, side, 0, gate=gate_sem).wait_send()
 
                     @pl.when(mine > other)
                     def _():
@@ -235,29 +277,36 @@
                         pl.semaphore_wait(turn, 1)
                         halo(t, c, side, 1).start()
 
-                halo(t, c, 1 - side, 0).wait_recv()
+                arrival(t, c, side, 0).wait_recv()
                 acc = lax.fori_loop(0, edge - 1, rim_tile, acc)
-                halo(t, c, 1 - side, 1).wait_recv()
                 if (t, c) == last and side is far:
-                    for k in range(1, n):
-                        moments(0, k).start()
-                acc = rim_tile(edge - 1, acc)
+                    for k in range(2, n, 2):
+                        to(duo.at[chip], k, 0).start()
+                if (t, c) == last and side is far:
+                    acc = split_tile(t, c, side, acc)
+                else:
+                    if side is far:
+                        arrival(t, c, side, 1).wait_recv()
+                    acc = rim_tile(edge - 1, acc)
                 if t + 1 < TERMS:
                     if (t + 1, c) == last and side is far:
-                        halo(t + 1, c, side, 0, 0, LEAD, gate_sem).start()
-                        if LEAD < inside:
-                            halo(t + 1, c, side, 0, LEAD, inside).start()
+                        halo(t + 1, c, side, 0, gate=gate_sem).start()
                         pl.when(mine >= other)(halo(t + 1, c, side, 1).start)
                     else:
-                        for part in range(2):
+                        for part in range(len(parts(side))):
                             halo(t + 1, c, side, part).start()
             total_row = jnp.sum(acc, axis=0, keepdims=True)
             for k in range(cc // LANES):
                 mom[me, t, pl.ds(c * (cc // LANES) + k, 1), :] = total_row[:, k * LANES:(k + 1) * LANES]
+            if t == TERMS - 1 and c == 0:
+                pair.wait_recv()
+                duo[chip] = mom[me, 0:TERMS - 1] + mom[lax.rem(me + partner, n), 0:TERMS - 1]
+            if t == TERMS - 2 and c + 1 == chunks:
+                pair.start()
             if t == 0:
                 spread(0 if c == 0 else 1, 1 if c + 1 < chunks else rounds)
     for k in range(1, n):
-        moments(1, k).start()
+        to(mom.at[me, TERMS - 1], k, 1).start()
 
     pltpu.make_async_remote_copy(
         src_ref=ext.at[0:TERMS - 1, :, pl.ds(0, 2 * rim)], dst_ref=ext.at[0:TERMS - 1, :, pl.ds(0, 2 * rim)],
@@ -266,13 +315,14 @@
     ).wait_send()
     for c in range(chunks):
         for side in (near, far):
-            held = LEAD if (TERMS - 1, c) == last and side is far else 0
-            halo(TERMS - 1, c, side, 0, held, BAND).wait_send()
-    for final in range(2):
-        moments(final, 1, 0, n - 1).wait()
-
-
-def finish(tb, mom, last_prev, last_cur, mom_hbm, row_sums, sem):
+            held = inside if (TERMS - 1, c) == last and side is far else 0
+            halo(TERMS - 1, c, side, 0, held, rim).wait_send()
+    pair.wait_send()
+    to(duo.at[pl.ds(0, n // 2 - 1)], 1, 0).wait()
+    to(mom.at[pl.ds(0, n - 1), TERMS - 1], 1, 1).wait()
+
+
+def finish(tb, mom, duo, last_prev, last_cur, mom_hbm, row_sums, sem):
     n, terms, lanes_of, _ = mom.shape
     _, chunks, _, cc = tb.shape
     copies = []
@@ -284,9 +334,10 @@
     for copy in copies:
         copy.start()
     for t in range(terms):
-        whole = mom[0, t]
-        for i in range(1, n):
-            whole = whole + mom[i, t]
+        kept, count = (mom, n) if t == terms - 1 else (duo, n // 2)
+        whole = kept[0, t]
+        for i in range(1, count):
+            whole = whole + kept[i, t]
         for k in range(lanes_of):
             row_sums[t:t + 1, k * LANES:(k + 1) * LANES] = whole[k:k + 1, :]
     copies.append(pltpu.make_async_copy(row_sums, mom_hbm, sem.at[2 * chunks]))
@@ -304,15 +355,16 @@
     vmem = pl.BlockSpec(memory_space=pltpu.VMEM)
     hbm = pl.BlockSpec(memory_space=pltpu.HBM)
     bf16, f32 = jnp.bfloat16, jnp.float32
-    grant = 67043328 - 4 * (2 * height * cols + TERMS * n * cols) - (64 << 10)
-    tb, mom = pl.pallas_call(
+    grant = 67043328 - 4 * (2 * height * cols + 2 * TERMS * n * cols) - (64 << 10)
+    tb, mom, duo = pl.pallas_call(
         functools.partial(kernel, n),
         out_shape=(
             pltpu.VMEM((2, chunks, height, cc), f32),
             pltpu.VMEM((n, TERMS, cols // LANES, LANES), f32),
+            pltpu.VMEM((n // 2, TERMS - 1, cols // LANES, LANES), f32),
         ),
         in_specs=[hbm] * 6,
-        out_specs=(vmem, vmem),
+        out_specs=(vmem, vmem, vmem),
         scratch_shapes=[
             pltpu.SMEM((rows, slots), jnp.int32),
             pltpu.VMEM((rows, w), f32),
@@ -321,11 +373,11 @@
             pltpu.VMEM((TERMS, chunks, height + 2 * BAND * w, cc), bf16),
             pltpu.VMEM((chunks, height, cc), f32),
             pltpu.VMEM((height, cols), bf16),
-            pltpu.SemaphoreType.DMA((8 + 2 * chunks,)),
+            pltpu.SemaphoreType.DMA((10 + 2 * chunks,)),
             pltpu.SemaphoreType.DMA,
-            pltpu.SemaphoreType.DMA((2, chunks, 2, 2)),
+            pltpu.SemaphoreType.DMA((2, chunks, 3)),
             pltpu.SemaphoreType.DMA,
-            pltpu.SemaphoreType.DMA((2,)),
+            pltpu.SemaphoreType.DMA((3,)),
             pltpu.SemaphoreType.REGULAR((max(1, (n // 2 - 1).bit_length()),)),
             pltpu.SemaphoreType.DMA,
             pltpu.SemaphoreType.REGULAR,
@@ -341,14 +393,14 @@
             jax.ShapeDtypeStruct((height, cols), f32),
             jax.ShapeDtypeStruct((TERMS, cols), f32),
         ),
-        in_specs=[vmem, vmem],
+        in_specs=[vmem, vmem, vmem],
         out_specs=(hbm, hbm, hbm),
         scratch_shapes=[
             pltpu.VMEM((TERMS, cols), f32),
             pltpu.SemaphoreType.DMA((2 * chunks + 1,)),
         ],
         compiler_params=pltpu.CompilerParams(vmem_limit_bytes=16 * 1024 * 1024),
-    )(tb, mom)
+    )(tb, mom, duo)
 
 
 def solution(mesh):

time: 54.7 us -> 54.6 us (level)
  no operation moved by 1% of the time
where the time goes in v3:
time: 54.6 us; the launch traced here: 54.4 us
  Pallas kernels  53.8 us (99%)
  between operations  0.64 us (1%)
    pallas_call x1, Pallas kernels, local(): pl.pallas_call(functools.partial(kernel, n), out_shape=(pltpu.VMEM((2, ch...  50.4 us
    pallas_call x1, Pallas kernels, local(): pl.pallas_call(finish, out_shape=(jax.ShapeDtypeStruct((height, cols), f3...  3.38 us

profile of v3, /device:TPU:0, one launch (start us, length us, event | category | flops | bytes accessed | tf_op | source)
XLA Modules:
  0.0 54.4 jit_solution(11634255842043111102)
XLA Ops:
  0.6 50.4 %shard_map.85 = (f32[2,2,2048,256]{3,2,1,0:T(8,128)S(1)}, f32[8,3,4,128]{3,2,1,0:T(4,128)S(1)}, f32[4,2,4,128]{3,2,1,0:T(4,128)S(1)}) custom-call(s32[16,9]{1,0:T(8,128)} %col_hbm.1, f32[16,128]{1,0:T(8,128)} %bitcast.1, bf16[16,9,128,128]{3,2,1,0:T(8,128)(2,1)} %h_hbm.1, bf16[2048,512]{1,0:T(8,128)(2,1)} %probe_hbm.1, f32[2048,512]{1,0:T(8,128)} %prev_hbm.1, ...), custom_call_target="tpu_custom_call" | custom-call | tf_op jit(solution)/shard_map/pallas_call | solution.py:359
  51.1 3.4 %shard_map.86 = (f32[2048,512]{1,0:T(8,128)}, f32[2048,512]{1,0:T(8,128)}, f32[3,512]{1,0:T(4,128)}) custom-call(f32[2,2,2048,256]{3,2,1,0:T(8,128)S(1)} %get-tuple-element.6.tb, f32[8,3,4,128]{3,2,1,0:T(4,128)S(1)} %get-tuple-element.7.mom, f32[4,2,4,128]{3,2,1,0:T(4,128)S(1)} %get-tuple-element.8.duo), custom_call_target="tpu_custom_call" | custom-call | tf_op jit(solution)/shard_map/pallas_call | solution.py:389
